TPU v7x, 32 devices: a whole 2x2x4 slice. The times are simulated.
32 devices in a mesh: samp: 8 (over z, x), win: 1, snp: 4 (over y, core).
Axes of the slice: x: 2, y: 2, z: 4, core: 2. Of those that a mesh axis runs over, the one named last changes fastest.
Arguments:
- dosages: bfloat16 [4096, 4096], P('samp', ('win', 'snp')), may hold values from 0 to 2
Outputs:
- r_squared: float32 [1, 4096, 4096], P('win', 'samp', 'snp')
- band_r_squared: float32 [1, 1024, 4096], P('win', 'samp', 'snp')
All inputs are finite; a program needn't handle non-finite values.
Results may differ from a plain program's by a relative error of at most 0.0003.
Values may be sent and summed in bfloat16 or wider, within the bound.
A program may use at most 128 MiB of HBM per device.

v0:
```python
import functools

import jax
import jax.numpy as jnp
from jax import lax
from jax.experimental import pallas as pl
from jax.experimental.pallas import tpu as pltpu
from jax.sharding import PartitionSpec as P

OV = 1024
VAR_FLOOR = 0.05
COLS = 2
PARTS = 2
MESH = pl.DeviceIdType.MESH


def plan(line):
    own = [(0, r, c) for r in range(line) for c in range(PARTS)]
    other = [(1, r, c) for r in range(line) for c in range(PARTS)]
    late = [v for v in other if v[1] in (1, 2) and v[2] == PARTS - 1]
    other = [v for v in other if v not in late]
    other = other[:-1] + [v for v in late if v[1] == 2] + other[-1:] + [v for v in late if v[1] == 1]
    lag = min(PARTS + 1, len(own))
    order = own[:lag]
    for k in range(lag, len(own)):
        order += [own[k], other[k - lag]]
    return order + other[len(own) - lag:]


def lookup(i, values):
    out = jnp.int32(0)
    for j, v in enumerate(values):
        if v:
            out = out + jnp.where(i == j, jnp.int32(v), jnp.int32(0))
    return out


def kernel(sizes, x_hbm, win_out, band_out, k_buf, j_buf, b_buf, k_stat, j_stat, b_stat,
           local_sem, k_recv, up_send, down_send, x_send, j_recv, j_send, b_recv, b_send, w_send, *band_wide):
    shard_count, windows, blocks, rows, width, jw, band, bw = sizes
    line = shard_count // COLS
    part_rows = rows // PARTS
    bits = blocks.bit_length() - 1
    chunks = shard_count * PARTS
    s = lax.axis_index("samp")
    n = lax.axis_index("snp")
    z = s // COLS
    x = s % COLS
    has_up = z < line - 1
    has_down = z > 0
    up = {"samp": jnp.minimum(s + COLS, shard_count - COLS + x)}
    down = {"samp": jnp.maximum(s - COLS, x)}
    across = {"samp": s + 1 - 2 * x}
    near = jnp.minimum(z, line - 1 - z)

    def bit(v, b):
        return (v // (1 << b)) % 2

    def flip(b):
        return {"snp": n + (1 << b) * (1 - 2 * bit(n, b))}

    j_home = (s * jw) // width
    j_off = pl.multiple_of((s * jw) % width, jw)
    b_home = (s * band) // width
    b_off = pl.multiple_of(((s * band) % width) // bw * bw, bw)
    j_rel = [(bit(n, b) + bit(j_home, b)) % 2 for b in range(bits)]
    b_rel = [(bit(n, b) + bit(b_home, b)) % 2 for b in range(bits)]

    def sends_on(rel, b):
        low = jnp.int32(0)
        for a in range(b + 1):
            low = low + rel[a]
        return low == 0

    def is_home(rel):
        total = jnp.int32(0)
        for r in rel:
            total = total + r
        return total == 0

    j_mine = is_home(j_rel)
    b_mine = is_home(b_rel)

    def k_copy(q, sem, to):
        return pltpu.make_async_remote_copy(
            src_ref=k_buf.at[q], dst_ref=k_buf.at[q], send_sem=sem.at[q], recv_sem=k_recv.at[q],
            device_id=to, device_id_type=MESH)

    def slice_copy(src, buf, q, send, recv, to):
        return pltpu.make_async_remote_copy(
            src_ref=src, dst_ref=buf.at[q], send_sem=send, recv_sem=recv.at[q],
            device_id=to, device_id_type=MESH)

    order = plan(line)
    band_sum = band_wide[0] if band_wide else band_out

    def item(o):
        side = lookup(o, [v[0] for v in order])
        r = lookup(o, [v[1] for v in order])
        c = lookup(o, [v[2] for v in order])
        odd = r % 2
        inner = z + jnp.where(odd == 1, 0 - (r + 1) // 2, r // 2)
        outer = jnp.where(z < line - 1 - z, r, line - 1 - r)
        zz = jnp.where(r <= 2 * near, inner, outer)
        xx = jnp.where(side == 1, 1 - x, x)
        return side, zz, c, (zz * COLS + xx) * PARTS + c

    def skips_x(zz, c):
        return (c == PARTS - 1) & ((zz == z + 1) | (zz == z - 1))

    for c in range(PARTS):
        pltpu.make_async_copy(x_hbm.at[pl.ds(c * part_rows, part_rows)],
                              k_buf.at[s * PARTS + c], local_sem.at[c]).start()

    barrier = pltpu.get_barrier_semaphore()

    def greet(to):
        pl.semaphore_signal(barrier, inc=1, device_id=to, device_id_type=MESH)

    pl.when(has_up)(lambda: greet(up))
    pl.when(has_down)(lambda: greet(down))
    greet(across)
    for b in range(bits):
        greet(flip(b))
    expected = 1 + bits
    if windows > 1:
        w = lax.axis_index("win")
        before = {"win": (w + windows - 1) % windows}
        after = {"win": (w + 1) % windows}
        greet(before)
        greet(after)
        expected += 2
    pl.semaphore_wait(barrier, expected + has_up.astype(jnp.int32) + has_down.astype(jnp.int32))

    k_stat[...] = jnp.zeros_like(k_stat)
    j_stat[...] = jnp.zeros_like(j_stat)
    b_stat[...] = jnp.zeros_like(b_stat)
    for c in range(PARTS):
        pltpu.make_async_copy(x_hbm.at[pl.ds(c * part_rows, part_rows)],
                              k_buf.at[s * PARTS + c], local_sem.at[c]).wait()

    last_own = max(i for i, v in enumerate(order) if v[0] == 0)
    cross_late = (s + 1 - 2 * x) * PARTS + PARTS - 1

    def take(o):
        side, zz, c, q = item(o)
        mine = (side == 0) & (zz == z)

        @pl.when(jnp.logical_not(mine))
        def _():
            k_copy(q, x_send, across).wait_recv()

        @pl.when((side == 0) & (zz <= z) & has_up)
        def _():
            k_copy(q, up_send, up).start()

        @pl.when((side == 0) & (zz >= z) & has_down)
        def _():
            k_copy(q, down_send, down).start()

        @pl.when((side == 0) & jnp.logical_not(skips_x(zz, c)))
        def _():
            k_copy(q, x_send, across).start()

        if line > 1:
            @pl.when((o == last_own) & has_up)
            def _():
                k_copy(cross_late, up_send, up).start()

            @pl.when((o == last_own) & has_down)
            def _():
                k_copy(cross_late, down_send, down).start()

        for b in reversed(range(bits)):
            @pl.when(j_mine)
            def _():
                slice_copy(k_buf.at[q, :, pl.ds(j_off, jw)], j_buf, q, j_send.at[b, q], j_recv, flip(b)).start()

            if windows == 1:
                @pl.when(b_mine)
                def _():
                    slice_copy(k_buf.at[q, :, pl.ds(b_off, bw)], b_buf, q, b_send.at[b, q], b_recv, flip(b)).start()
        if windows > 1:
            @pl.when(b_mine)
            def _():
                slice_copy(k_buf.at[q, :, pl.ds(b_off, bw)], b_buf, q, w_send.at[q], b_recv, before).start()

    def j_arrive(q):
        slice_copy(k_buf.at[q, :, pl.ds(j_off, jw)], j_buf, q, j_send.at[0, q], j_recv, flip(0)).wait_recv()

    def b_arrive(q):
        slice_copy(k_buf.at[q, :, pl.ds(b_off, bw)], b_buf, q, b_send.at[0, q], b_recv, flip(0)).wait_recv()

    def relay(o):
        _, _, _, q = item(o)

        @pl.when(jnp.logical_not(j_mine))
        def _():
            j_arrive(q)
            for b in reversed(range(bits)):
                @pl.when(sends_on(j_rel, b))
                def _():
                    slice_copy(j_buf.at[q], j_buf, q, j_send.at[b, q], j_recv, flip(b)).start()

        @pl.when(j_mine)
        def _():
            j_buf[q] = k_buf[q, :, pl.ds(j_off, jw)]

        def pass_band():
            b_arrive(q)
            for b in reversed(range(bits)):
                @pl.when(sends_on(b_rel, b))
                def _():
                    slice_copy(b_buf.at[q], b_buf, q, b_send.at[b, q], b_recv, flip(b)).start()

        if windows > 1:
            pass_band()
        else:
            pl.when(jnp.logical_not(b_mine))(pass_band)

            @pl.when(b_mine)
            def _():
                b_buf[q] = k_buf[q, :, pl.ds(b_off, bw)]

    def add_stats(stat, block):
        wide = block.astype(jnp.float32).reshape(part_rows // 8, 8, block.shape[-1])
        stat[0] += jnp.sum(wide, axis=0)
        stat[1] += jnp.sum(wide * wide, axis=0)

    def pair(a, b):
        return lax.dot_general(a, b, (((0,), (0,)), ((), ())), preferred_element_type=jnp.float32)

    def compute(o):
        _, _, _, q = item(o)
        whole = k_buf[q]
        j_cols = j_buf[q]
        b_cols = b_buf[q]
        add_stats(k_stat, whole)
        add_stats(j_stat, j_cols)
        add_stats(b_stat, b_cols)

        @pl.when(o == 0)
        def _():
            win_out[0] = pair(j_cols, whole)
            band_sum[0] = pair(b_cols, whole)

        @pl.when(o > 0)
        def _():
            win_out[0] += pair(j_cols, whole)
            band_sum[0] += pair(b_cols, whole)

    def step(o, carry):
        @pl.when(o < chunks)
        def _():
            take(o)

        @pl.when((o >= 2) & (o < chunks + 2))
        def _():
            relay(o - 2)

        @pl.when(o >= 3)
        def _():
            compute(o - 3)

        return carry

    lax.fori_loop(0, chunks + 3, step, 0)

    count = jnp.float32(rows * shard_count)

    def moments(total, square):
        mean = total / count
        return mean, 1.0 / jnp.maximum(square / count - mean * mean, VAR_FLOOR)

    row_mean, row_inv = moments(jnp.sum(k_stat[0], axis=0, keepdims=True), jnp.sum(k_stat[1], axis=0, keepdims=True))

    def finish(out, stat, height):
        mean, inv = moments(jnp.sum(stat[0].T, axis=1, keepdims=True), jnp.sum(stat[1].T, axis=1, keepdims=True))
        for a in range(0, height, 64):
            e = min(a + 64, height)
            covar = out[0, a:e] / count - mean[a:e] * row_mean
            out[0, a:e] = covar * covar * (inv[a:e] * row_inv)

    finish(win_out, j_stat, jw)
    finish(band_sum, b_stat, bw)
    if band_wide:
        band_out[0] = band_sum[0, pl.ds(pl.multiple_of((s * band) % bw, band), band)]

    def drain(o, carry):
        side, zz, c, q = item(o)

        @pl.when((side == 0) & (zz <= z) & has_up)
        def _():
            k_copy(q, up_send, up).wait_send()

        @pl.when((side == 0) & (zz >= z) & has_down)
        def _():
            k_copy(q, down_send, down).wait_send()

        @pl.when((side == 0) & jnp.logical_not(skips_x(zz, c)))
        def _():
            k_copy(q, x_send, across).wait_send()

        for b in range(bits):
            @pl.when(sends_on(j_rel, b))
            def _():
                slice_copy(j_buf.at[q], j_buf, q, j_send.at[b, q], j_recv, flip(b)).wait_send()

            @pl.when(sends_on(b_rel, b))
            def _():
                slice_copy(b_buf.at[q], b_buf, q, b_send.at[b, q], b_recv, flip(b)).wait_send()
        if windows > 1:
            @pl.when(b_mine)
            def _():
                slice_copy(b_buf.at[q], b_buf, q, w_send.at[q], b_recv, before).wait_send()
        return carry

    lax.fori_loop(0, chunks, drain, 0)
    if line > 1:
        @pl.when(has_up)
        def _():
            k_copy(cross_late, up_send, up).wait_send()

        @pl.when(has_down)
        def _():
            k_copy(cross_late, down_send, down).wait_send()


def shards(dosages):
    rows, width = dosages.shape
    shard_count = lax.axis_size("samp")
    windows = lax.axis_size("win")
    blocks = lax.axis_size("snp")
    jw = width * blocks // shard_count
    band = OV // shard_count
    bw = max(band, 128)
    bits = blocks.bit_length() - 1
    chunks = shard_count * PARTS
    part_rows = rows // PARTS
    sizes = (shard_count, windows, blocks, rows, width, jw, band, bw)
    dma = pltpu.SemaphoreType.DMA
    return pl.pallas_call(
        functools.partial(kernel, sizes),
        out_shape=(
            jax.ShapeDtypeStruct((1, jw, width), jnp.float32),
            jax.ShapeDtypeStruct((1, band, width), jnp.float32),
        ),
        in_specs=[pl.BlockSpec(memory_space=pl.ANY)],
        out_specs=[pl.BlockSpec(memory_space=pltpu.VMEM)] * 2,
        scratch_shapes=[
            pltpu.VMEM((chunks, part_rows, width), jnp.bfloat16),
            pltpu.VMEM((chunks, part_rows, jw), jnp.bfloat16),
            pltpu.VMEM((chunks, part_rows, bw), jnp.bfloat16),
            pltpu.VMEM((2, 8, width), jnp.float32),
            pltpu.VMEM((2, 8, jw), jnp.float32),
            pltpu.VMEM((2, 8, bw), jnp.float32),
            dma((PARTS,)),
            dma((chunks,)), dma((chunks,)), dma((chunks,)), dma((chunks,)),
            dma((chunks,)), dma((bits, chunks)),
            dma((chunks,)), dma((bits, chunks)), dma((chunks,)),
        ] + ([pltpu.VMEM((1, bw, width), jnp.float32)] if bw != band else []),
        compiler_params=pltpu.CompilerParams(
            collective_id=0, has_side_effects=True, vmem_limit_bytes=67043328
        ),
    )(dosages)


def solution(mesh):
    return jax.shard_map(
        shards,
        mesh=mesh,
        in_specs=(P("samp", ("win", "snp")),),
        out_specs=(P("win", "samp", "snp"), P("win", "samp", "snp")),
        check_vma=False,
    )
```

profile of v0, /device:TPU:15, one launch (start us, length us, event | category | flops | bytes accessed | tf_op | source)
XLA Modules:
  0.0 109.2 jit_solution(10130384724290694615)
XLA Ops:
  0.6 104.6 %shard_map.30 = (f32[1,512,1024]{2,1,0:T(8,128)}, f32[1,128,1024]{2,1,0:T(8,128)}) custom-call(bf16[512,1024]{1,0:T(8,128)(2,1)} %x_hbm.1), custom_call_target="tpu_custom_call" | custom-call | tf_op jit(solution)/shard_map/pallas_call | solution.py:342
  105.2 0.0 copy-start
  105.2 3.2 %copy.5 = f32[1,512,1024]{2,1,0:T(8,128)} copy(f32[1,512,1024]{2,1,0:T(8,128)} %get-tuple-element.4) | data formatting | bytes 4194304
  108.4 0.0 copy-done
  108.4 0.8 copy.6
Async XLA Ops:
  105.2 3.2 %copy-start = (f32[1,128,1024]{2,1,0:T(8,128)S(1)}, f32[1,128,1024]{2,1,0:T(8,128)}, u32[]{:S(2)}) copy-start(f32[1,128,1024]{2,1,0:T(8,128)} %get-tuple-element.5) | copy-start | bytes 1572868
where the time goes:
time: 109 us
  Pallas kernels  105 us (96%)
  local copies, waits for them, and re-layouts  4.01 us (4%)
    pallas_call x1, Pallas kernels, shards(): pl.pallas_call(functools.partial(kernel, sizes), out_shape=(jax.ShapeDtyp...  105 us
    unnamed x4, local copies, waits for them, and re-layouts  4.01 us

commit v1 on v0

--- a/solution.py
+++ b/solution.py
@@ -1,4 +1,5 @@
 import functools
+import heapq
 
 import jax
 import jax.numpy as jnp
@@ -10,21 +11,60 @@
 OV = 1024
 VAR_FLOOR = 0.05
 COLS = 2
-PARTS = 2
+PARTS = 4
+LATE = PARTS // 2
 MESH = pl.DeviceIdType.MESH
 
 
+def by_z(z, zz, c):
+    return c >= LATE and abs(z - zz) == 1
+
+
+def sends(line, z, item):
+    side, zz, c = item
+    out = []
+    if side == 0:
+        if zz <= z and z < line - 1:
+            out.append((1, item))
+        if zz >= z and z > 0:
+            out.append((-1, item))
+        if not by_z(z, zz, c):
+            out.append((0, item))
+        if c == PARTS - 1:
+            for way, far in ((-1, line - 1), (1, 0)):
+                if zz == far and 0 <= z + way < line and last_on(line, z, way):
+                    out += [(way, (1, z, k)) for k in range(LATE, PARTS)]
+    elif zz == z and c >= LATE:
+        for way in (-1, 1):
+            if 0 <= z + way < line and not last_on(line, z, way):
+                out.append((way, item))
+    return out
+
+
+def last_on(line, z, way):
+    return z < line // 2 if way < 0 else z >= line // 2
+
+
 def plan(line):
-    own = [(0, r, c) for r in range(line) for c in range(PARTS)]
-    other = [(1, r, c) for r in range(line) for c in range(PARTS)]
-    late = [v for v in other if v[1] in (1, 2) and v[2] == PARTS - 1]
-    other = [v for v in other if v not in late]
-    other = other[:-1] + [v for v in late if v[1] == 2] + other[-1:] + [v for v in late if v[1] == 1]
-    lag = min(PARTS + 1, len(own))
-    order = own[:lag]
-    for k in range(lag, len(own)):
-        order += [own[k], other[k - lag]]
-    return order + other[len(own) - lag:]
+    hop = 1.0
+    lag = 0.35
+    events = [(0.0, z * PARTS + c, z, (0, z, c)) for z in range(line) for c in range(PARTS)]
+    heapq.heapify(events)
+    free = {}
+    order = [[] for _ in range(line)]
+    count = line * PARTS
+    while events:
+        t, _, z, item = heapq.heappop(events)
+        order[z].append(item)
+        for way, (side, zz, c) in sends(line, z, item):
+            begin = max(free.get((z, way), 0.0), t)
+            free[z, way] = begin + hop
+            moved = (side, zz, c) if way else (1 - side, zz, c)
+            heapq.heappush(events, (begin + hop + lag, count, z + way, moved))
+            count += 1
+    for z in range(line // 2, line):
+        order[z] = [(side, line - 1 - zz, c) for side, zz, c in order[line - 1 - z]]
+    return order
 
 
 def lookup(i, values):
@@ -51,7 +91,6 @@
     up = {"samp": jnp.minimum(s + COLS, shard_count - COLS + x)}
     down = {"samp": jnp.maximum(s - COLS, x)}
     across = {"samp": s + 1 - 2 * x}
-    near = jnp.minimum(z, line - 1 - z)
 
     def bit(v, b):
         return (v // (1 << b)) % 2
@@ -93,20 +132,29 @@
 
     order = plan(line)
     band_sum = band_wide[0] if band_wide else band_out
+    low = z < line // 2
+    near_z = jnp.where(low, z, line - 1 - z)
 
     def item(o):
-        side = lookup(o, [v[0] for v in order])
-        r = lookup(o, [v[1] for v in order])
-        c = lookup(o, [v[2] for v in order])
-        odd = r % 2
-        inner = z + jnp.where(odd == 1, 0 - (r + 1) // 2, r // 2)
-        outer = jnp.where(z < line - 1 - z, r, line - 1 - r)
-        zz = jnp.where(r <= 2 * near, inner, outer)
+        code = jnp.int32(0)
+        for half in range((line + 1) // 2):
+            mine = lookup(o, [(side * line + zz) * PARTS + c for side, zz, c in order[half]])
+            code = code + jnp.where(near_z == half, mine, 0)
+        c = code % PARTS
+        zz = (code // PARTS) % line
+        side = code // (PARTS * line)
+        zz = jnp.where(low, zz, line - 1 - zz)
         xx = jnp.where(side == 1, 1 - x, x)
         return side, zz, c, (zz * COLS + xx) * PARTS + c
 
     def skips_x(zz, c):
-        return (c == PARTS - 1) & ((zz == z + 1) | (zz == z - 1))
+        return (c >= LATE) & ((zz == z + 1) | (zz == z - 1))
+
+    crossed = [(s + 1 - 2 * x) * PARTS + c for c in range(LATE, PARTS)]
+    up_last = has_up & (z >= line // 2)
+    down_last = has_down & (z < line // 2)
+    up_soon = has_up & (z < line // 2)
+    down_soon = has_down & (z >= line // 2)
 
     for c in range(PARTS):
         pltpu.make_async_copy(x_hbm.at[pl.ds(c * part_rows, part_rows)],
@@ -135,17 +183,18 @@
     k_stat[...] = jnp.zeros_like(k_stat)
     j_stat[...] = jnp.zeros_like(j_stat)
     b_stat[...] = jnp.zeros_like(b_stat)
-    for c in range(PARTS):
-        pltpu.make_async_copy(x_hbm.at[pl.ds(c * part_rows, part_rows)],
-                              k_buf.at[s * PARTS + c], local_sem.at[c]).wait()
-
-    last_own = max(i for i, v in enumerate(order) if v[0] == 0)
-    cross_late = (s + 1 - 2 * x) * PARTS + PARTS - 1
+    win_out[...] = jnp.zeros_like(win_out)
+    band_sum[...] = jnp.zeros_like(band_sum)
 
     def take(o):
         side, zz, c, q = item(o)
         mine = (side == 0) & (zz == z)
 
+        @pl.when(mine)
+        def _():
+            pltpu.make_async_copy(x_hbm.at[pl.ds(c * part_rows, part_rows)],
+                                  k_buf.at[s * PARTS + c], local_sem.at[c]).wait()
+
         @pl.when(jnp.logical_not(mine))
         def _():
             k_copy(q, x_send, across).wait_recv()
@@ -163,13 +212,26 @@
             k_copy(q, x_send, across).start()
 
         if line > 1:
-            @pl.when((o == last_own) & has_up)
-            def _():
-                k_copy(cross_late, up_send, up).start()
-
-            @pl.when((o == last_own) & has_down)
-            def _():
-                k_copy(cross_late, down_send, down).start()
+            passes = (side == 1) & (zz == z) & (c >= LATE)
+            ends = (side == 0) & (c == PARTS - 1)
+
+            @pl.when(passes & up_soon)
+            def _():
+                k_copy(q, up_send, up).start()
+
+            @pl.when(passes & down_soon)
+            def _():
+                k_copy(q, down_send, down).start()
+
+            @pl.when(ends & (zz == 0) & up_last)
+            def _():
+                for k in crossed:
+                    k_copy(k, up_send, up).start()
+
+            @pl.when(ends & (zz == line - 1) & down_last)
+            def _():
+                for k in crossed:
+                    k_copy(k, down_send, down).start()
 
         for b in reversed(range(bits)):
             @pl.when(j_mine)
@@ -239,15 +301,8 @@
         add_stats(j_stat, j_cols)
         add_stats(b_stat, b_cols)
 
-        @pl.when(o == 0)
-        def _():
-            win_out[0] = pair(j_cols, whole)
-            band_sum[0] = pair(b_cols, whole)
-
-        @pl.when(o > 0)
-        def _():
-            win_out[0] += pair(j_cols, whole)
-            band_sum[0] += pair(b_cols, whole)
+        win_out[0] += pair(j_cols, whole)
+        band_sum[0] += pair(b_cols, whole)
 
     def step(o, carry):
         @pl.when(o < chunks)
@@ -317,13 +372,14 @@
 
     lax.fori_loop(0, chunks, drain, 0)
     if line > 1:
-        @pl.when(has_up)
-        def _():
-            k_copy(cross_late, up_send, up).wait_send()
-
-        @pl.when(has_down)
-        def _():
-            k_copy(cross_late, down_send, down).wait_send()
+        for k in crossed:
+            @pl.when(has_up)
+            def _():
+                k_copy(k, up_send, up).wait_send()
+
+            @pl.when(has_down)
+            def _():
+                k_copy(k, down_send, down).wait_send()
 
 
 def shards(dosages):

time: 109 us -> 116 us (1.064)
  the two profiles are of different devices: /device:TPU:15 before, /device:TPU:5 now
where the time goes in v1:
time: 116 us
  Pallas kernels  111 us (96%)
  local copies, waits for them, and re-layouts  4.01 us (3%)
    pallas_call x1, Pallas kernels, shards(): pl.pallas_call(functools.partial(kernel, sizes), out_shape=(jax.ShapeDtyp...  111 us
    unnamed x4, local copies, waits for them, and re-layouts  4.01 us

profile of v1, /device:TPU:5, one launch (start us, length us, event | category | flops | bytes accessed | tf_op | source)
XLA Modules:
  0.0 116.0 jit_solution(108927688765175945)
XLA Ops:
  0.6 111.3 %shard_map.30 = (f32[1,512,1024]{2,1,0:T(8,128)}, f32[1,128,1024]{2,1,0:T(8,128)}) custom-call(bf16[512,1024]{1,0:T(8,128)(2,1)} %x_hbm.1), custom_call_target="tpu_custom_call" | custom-call | tf_op jit(solution)/shard_map/pallas_call | solution.py:398
  111.9 0.0 copy-start
  112.0 3.2 %copy.5 = f32[1,512,1024]{2,1,0:T(8,128)} copy(f32[1,512,1024]{2,1,0:T(8,128)} %get-tuple-element.4) | data formatting | bytes 4194304
  115.2 0.0 copy-done
  115.2 0.8 copy.6
Async XLA Ops:
  111.9 3.2 %copy-start = (f32[1,128,1024]{2,1,0:T(8,128)S(1)}, f32[1,128,1024]{2,1,0:T(8,128)}, u32[]{:S(2)}) copy-start(f32[1,128,1024]{2,1,0:T(8,128)} %get-tuple-element.5) | copy-start | bytes 1572868

commit v2 on v1

--- a/solution.py
+++ b/solution.py
@@ -13,6 +13,8 @@
 COLS = 2
 PARTS = 4
 LATE = PARTS // 2
+PASS = 2
+USE = 4
 MESH = pl.DeviceIdType.MESH
 
 
@@ -122,7 +124,7 @@
 
     def k_copy(q, sem, to):
         return pltpu.make_async_remote_copy(
-            src_ref=k_buf.at[q], dst_ref=k_buf.at[q], send_sem=sem.at[q], recv_sem=k_recv.at[q],
+            src_ref=k_buf.at[q], dst_ref=k_buf.at[q], send_sem=sem, recv_sem=k_recv.at[q],
             device_id=to, device_id_type=MESH)
 
     def slice_copy(src, buf, q, send, recv, to):
@@ -186,8 +188,7 @@
     win_out[...] = jnp.zeros_like(win_out)
     band_sum[...] = jnp.zeros_like(band_sum)
 
-    def take(o):
-        side, zz, c, q = item(o)
+    def take(side, zz, c, q):
         mine = (side == 0) & (zz == z)
 
         @pl.when(mine)
@@ -236,50 +237,57 @@
         for b in reversed(range(bits)):
             @pl.when(j_mine)
             def _():
-                slice_copy(k_buf.at[q, :, pl.ds(j_off, jw)], j_buf, q, j_send.at[b, q], j_recv, flip(b)).start()
+                slice_copy(k_buf.at[q, :, pl.ds(j_off, jw)], j_buf, q, j_send.at[b], j_recv, flip(b)).start()
 
             if windows == 1:
                 @pl.when(b_mine)
                 def _():
-                    slice_copy(k_buf.at[q, :, pl.ds(b_off, bw)], b_buf, q, b_send.at[b, q], b_recv, flip(b)).start()
+                    slice_copy(k_buf.at[q, :, pl.ds(b_off, bw)], b_buf, q, b_send.at[b], b_recv, flip(b)).start()
         if windows > 1:
             @pl.when(b_mine)
             def _():
-                slice_copy(k_buf.at[q, :, pl.ds(b_off, bw)], b_buf, q, w_send.at[q], b_recv, before).start()
+                slice_copy(k_buf.at[q, :, pl.ds(b_off, bw)], b_buf, q, w_send, b_recv, before).start()
 
     def j_arrive(q):
-        slice_copy(k_buf.at[q, :, pl.ds(j_off, jw)], j_buf, q, j_send.at[0, q], j_recv, flip(0)).wait_recv()
+        slice_copy(k_buf.at[q, :, pl.ds(j_off, jw)], j_buf, q, j_send.at[0], j_recv, flip(0)).wait_recv()
 
     def b_arrive(q):
-        slice_copy(k_buf.at[q, :, pl.ds(b_off, bw)], b_buf, q, b_send.at[0, q], b_recv, flip(0)).wait_recv()
-
-    def relay(o):
-        _, _, _, q = item(o)
-
-        @pl.when(jnp.logical_not(j_mine))
+        slice_copy(k_buf.at[q, :, pl.ds(b_off, bw)], b_buf, q, b_send.at[0], b_recv, flip(0)).wait_recv()
+
+    j_passes = (j_rel[0] == 0) & jnp.logical_not(j_mine)
+    b_passes = b_rel[0] == 0 if windows > 1 else (b_rel[0] == 0) & jnp.logical_not(b_mine)
+
+    def forward(q):
+        @pl.when(j_passes)
         def _():
             j_arrive(q)
             for b in reversed(range(bits)):
                 @pl.when(sends_on(j_rel, b))
                 def _():
-                    slice_copy(j_buf.at[q], j_buf, q, j_send.at[b, q], j_recv, flip(b)).start()
-
-        @pl.when(j_mine)
-        def _():
-            j_buf[q] = k_buf[q, :, pl.ds(j_off, jw)]
-
-        def pass_band():
+                    slice_copy(j_buf.at[q], j_buf, q, j_send.at[b], j_recv, flip(b)).start()
+
+        @pl.when(b_passes)
+        def _():
             b_arrive(q)
             for b in reversed(range(bits)):
                 @pl.when(sends_on(b_rel, b))
                 def _():
-                    slice_copy(b_buf.at[q], b_buf, q, b_send.at[b, q], b_recv, flip(b)).start()
-
-        if windows > 1:
-            pass_band()
-        else:
-            pl.when(jnp.logical_not(b_mine))(pass_band)
-
+                    slice_copy(b_buf.at[q], b_buf, q, b_send.at[b], b_recv, flip(b)).start()
+
+    def ready(q):
+        @pl.when(j_rel[0] != 0)
+        def _():
+            j_arrive(q)
+
+        @pl.when(j_mine)
+        def _():
+            j_buf[q] = k_buf[q, :, pl.ds(j_off, jw)]
+
+        @pl.when(b_rel[0] != 0)
+        def _():
+            b_arrive(q)
+
+        if windows == 1:
             @pl.when(b_mine)
             def _():
                 b_buf[q] = k_buf[q, :, pl.ds(b_off, bw)]
@@ -292,8 +300,8 @@
     def pair(a, b):
         return lax.dot_general(a, b, (((0,), (0,)), ((), ())), preferred_element_type=jnp.float32)
 
-    def compute(o):
-        _, _, _, q = item(o)
+    def compute(q):
+        ready(q)
         whole = k_buf[q]
         j_cols = j_buf[q]
         b_cols = b_buf[q]
@@ -304,22 +312,24 @@
         win_out[0] += pair(j_cols, whole)
         band_sum[0] += pair(b_cols, whole)
 
-    def step(o, carry):
+    def step(o, held):
+        side, zz, c, q = item(o)
+
         @pl.when(o < chunks)
         def _():
-            take(o)
-
-        @pl.when((o >= 2) & (o < chunks + 2))
-        def _():
-            relay(o - 2)
-
-        @pl.when(o >= 3)
-        def _():
-            compute(o - 3)
-
-        return carry
-
-    lax.fori_loop(0, chunks + 3, step, 0)
+            take(side, zz, c, q)
+
+        @pl.when((o >= PASS) & (o < chunks + PASS))
+        def _():
+            forward(held[PASS - 1])
+
+        @pl.when(o >= USE)
+        def _():
+            compute(held[USE - 1])
+
+        return (q, *held[:-1])
+
+    lax.fori_loop(0, chunks + USE, step, (jnp.int32(0),) * USE)
 
     count = jnp.float32(rows * shard_count)
 
@@ -341,45 +351,35 @@
     if band_wide:
         band_out[0] = band_sum[0, pl.ds(pl.multiple_of((s * band) % bw, band), band)]
 
-    def drain(o, carry):
-        side, zz, c, q = item(o)
-
-        @pl.when((side == 0) & (zz <= z) & has_up)
-        def _():
-            k_copy(q, up_send, up).wait_send()
-
-        @pl.when((side == 0) & (zz >= z) & has_down)
-        def _():
-            k_copy(q, down_send, down).wait_send()
-
-        @pl.when((side == 0) & jnp.logical_not(skips_x(zz, c)))
-        def _():
-            k_copy(q, x_send, across).wait_send()
-
-        for b in range(bits):
-            @pl.when(sends_on(j_rel, b))
-            def _():
-                slice_copy(j_buf.at[q], j_buf, q, j_send.at[b, q], j_recv, flip(b)).wait_send()
-
-            @pl.when(sends_on(b_rel, b))
-            def _():
-                slice_copy(b_buf.at[q], b_buf, q, b_send.at[b, q], b_recv, flip(b)).wait_send()
-        if windows > 1:
-            @pl.when(b_mine)
-            def _():
-                slice_copy(b_buf.at[q], b_buf, q, w_send.at[q], b_recv, before).wait_send()
-        return carry
-
-    lax.fori_loop(0, chunks, drain, 0)
-    if line > 1:
-        for k in crossed:
-            @pl.when(has_up)
-            def _():
-                k_copy(k, up_send, up).wait_send()
-
-            @pl.when(has_down)
-            def _():
-                k_copy(k, down_send, down).wait_send()
+    def sent(buf, number, sem):
+        part = buf.at[pl.ds(0, number)]
+        pltpu.make_async_remote_copy(
+            src_ref=part, dst_ref=part, send_sem=sem, recv_sem=k_recv.at[0],
+            device_id=across, device_id_type=MESH).wait_send()
+
+    for zz in range(line):
+        over = sum(not by_z(zz, a, c) for a in range(line) for c in range(PARTS))
+
+        @pl.when(z == zz)
+        def _():
+            if zz < line - 1:
+                sent(k_buf, (zz + 1) * PARTS + PARTS - LATE, up_send)
+            if zz > 0:
+                sent(k_buf, (line - zz) * PARTS + PARTS - LATE, down_send)
+            sent(k_buf, over, x_send)
+
+    for b in range(bits):
+        @pl.when(sends_on(j_rel, b))
+        def _():
+            sent(j_buf, chunks, j_send.at[b])
+
+        @pl.when(sends_on(b_rel, b))
+        def _():
+            sent(b_buf, chunks, b_send.at[b])
+    if windows > 1:
+        @pl.when(b_mine)
+        def _():
+            sent(b_buf, chunks, w_send)
 
 
 def shards(dosages):
@@ -411,9 +411,9 @@
             pltpu.VMEM((2, 8, jw), jnp.float32),
             pltpu.VMEM((2, 8, bw), jnp.float32),
             dma((PARTS,)),
-            dma((chunks,)), dma((chunks,)), dma((chunks,)), dma((chunks,)),
-            dma((chunks,)), dma((bits, chunks)),
-            dma((chunks,)), dma((bits, chunks)), dma((chunks,)),
+            dma((chunks,)), dma, dma, dma,
+            dma((chunks,)), dma((bits,)),
+            dma((chunks,)), dma((bits,)), dma,
         ] + ([pltpu.VMEM((1, bw, width), jnp.float32)] if bw != band else []),
         compiler_params=pltpu.CompilerParams(
             collective_id=0, has_side_effects=True, vmem_limit_bytes=67043328

time: 116 us -> 98.4 us (0.85)
  Pallas kernels: 111 us -> 93.6 us
    pallas_call x1, Pallas kernels: 111 us -> 93.6 us  [shards(): pl.pallas_call(functools.partial(kernel, sizes), out_shape=(jax.ShapeDtyp...]
where the time goes in v2:
time: 98.4 us; the launch traced here: 98.2 us
  Pallas kernels  93.6 us (95%)
  local copies, waits for them, and re-layouts  4.01 us (4%)
    pallas_call x1, Pallas kernels, shards(): pl.pallas_call(functools.partial(kernel, sizes), out_shape=(jax.ShapeDtyp...  93.6 us
    unnamed x4, local copies, waits for them, and re-layouts  4.01 us

profile of v2, /device:TPU:5, one launch (start us, length us, event | category | flops | bytes accessed | tf_op | source)
XLA Modules:
  0.0 98.2 jit_solution(14149010733377030526)
XLA Ops:
  0.6 93.6 %shard_map.30 = (f32[1,512,1024]{2,1,0:T(8,128)}, f32[1,128,1024]{2,1,0:T(8,128)}) custom-call(bf16[512,1024]{1,0:T(8,128)(2,1)} %x_hbm.1), custom_call_target="tpu_custom_call" | custom-call | tf_op jit(solution)/shard_map/pallas_call | solution.py:398
  94.2 0.0 copy-start
  94.2 3.2 %copy.5 = f32[1,512,1024]{2,1,0:T(8,128)} copy(f32[1,512,1024]{2,1,0:T(8,128)} %get-tuple-element.4) | data formatting | bytes 4194304
  97.4 0.0 copy-done
  97.4 0.8 copy.6
Async XLA Ops:
  94.2 3.2 %copy-start = (f32[1,128,1024]{2,1,0:T(8,128)S(1)}, f32[1,128,1024]{2,1,0:T(8,128)}, u32[]{:S(2)}) copy-start(f32[1,128,1024]{2,1,0:T(8,128)} %get-tuple-element.5) | copy-start | bytes 1572868

commit v3 on v2

--- a/solution.py
+++ b/solution.py
@@ -15,6 +15,8 @@
 LATE = PARTS // 2
 PASS = 2
 USE = 4
+HEAD_START = 6000
+LAST = 2
 MESH = pl.DeviceIdType.MESH
 
 
@@ -182,6 +184,8 @@
         expected += 2
     pl.semaphore_wait(barrier, expected + has_up.astype(jnp.int32) + has_down.astype(jnp.int32))
 
+    pl.when((n > 0) & (n < blocks - 1))(lambda: pl.delay(HEAD_START))
+
     k_stat[...] = jnp.zeros_like(k_stat)
     j_stat[...] = jnp.zeros_like(j_stat)
     b_stat[...] = jnp.zeros_like(b_stat)
@@ -312,24 +316,32 @@
         win_out[0] += pair(j_cols, whole)
         band_sum[0] += pair(b_cols, whole)
 
+    def place(o):
+        return item(o)[3]
+
+    def summed(o):
+        closing = jnp.maximum(0, o - (chunks - 1 - 2 * (USE - LAST))) // 2
+        return jnp.maximum(0, o + 1 - jnp.maximum(LAST, USE - closing))
+
     def step(o, held):
         side, zz, c, q = item(o)
-
-        @pl.when(o < chunks)
-        def _():
-            take(side, zz, c, q)
-
-        @pl.when((o >= PASS) & (o < chunks + PASS))
+        take(side, zz, c, q)
+
+        @pl.when(o >= PASS)
         def _():
             forward(held[PASS - 1])
 
-        @pl.when(o >= USE)
-        def _():
-            compute(held[USE - 1])
-
+        lax.fori_loop(summed(o - 1), summed(o), lambda i, _: compute(place(i)), None)
         return (q, *held[:-1])
 
-    lax.fori_loop(0, chunks + USE, step, (jnp.int32(0),) * USE)
+    held = lax.fori_loop(0, chunks, step, (jnp.int32(0),) * PASS)
+    for k in reversed(range(PASS)):
+        forward(held[k])
+
+    def rest(i, _):
+        compute(place(i))
+
+    lax.fori_loop(chunks - LAST, chunks, rest, None)
 
     count = jnp.float32(rows * shard_count)
 
@@ -416,7 +428,7 @@
             dma((chunks,)), dma((bits,)), dma,
         ] + ([pltpu.VMEM((1, bw, width), jnp.float32)] if bw != band else []),
         compiler_params=pltpu.CompilerParams(
-            collective_id=0, has_side_effects=True, vmem_limit_bytes=67043328
+            collective_id=0, has_side_effects=True, vmem_limit_bytes=24 * 2**20
         ),
     )(dosages)
 

time: 98.4 us -> 94 us (0.955)
  Pallas kernels: 93.6 us -> 89.4 us
    pallas_call x1, Pallas kernels: 93.6 us -> 89.4 us  [shards(): pl.pallas_call(functools.partial(kernel, sizes), out_shape=(jax.ShapeDtyp...]
where the time goes in v3:
time: 94 us; the launch traced here: 93.3 us
  Pallas kernels  89.4 us (95%)
  local copies, waits for them, and re-layouts  3.33 us (4%)
    pallas_call x1, Pallas kernels, shards(): pl.pallas_call(functools.partial(kernel, sizes), out_shape=(jax.ShapeDtyp...  89.4 us
    unnamed x4, local copies, waits for them, and re-layouts  3.33 us

profile of v3, /device:TPU:5, one launch (start us, length us, event | category | flops | bytes accessed | tf_op | source)
XLA Modules:
  0.0 93.3 jit_solution(5166868362365349823)
XLA Ops:
  0.6 0.0 copy-start
  0.6 1.2 %copy-done = bf16[512,1024]{1,0:T(8,128)(2,1)S(1)} copy-done((bf16[512,1024]{1,0:T(8,128)(2,1)S(1)}, bf16[512,1024]{1,0:T(8,128)(2,1)}, u32[]{:S(2)}) %copy-start) | copy-done | bytes 1048600
  1.9 89.4 %shard_map.30 = (f32[1,512,1024]{2,1,0:T(8,128)S(1)}, f32[1,128,1024]{2,1,0:T(8,128)S(1)}) custom-call(bf16[512,1024]{1,0:T(8,128)(2,1)S(1)} %copy-done), custom_call_target="tpu_custom_call" | custom-call | tf_op jit(solution)/shard_map/pallas_call | solution.py:410
  91.2 1.3 %copy.5 = f32[1,512,1024]{2,1,0:T(8,128)} copy(f32[1,512,1024]{2,1,0:T(8,128)S(1)} %get-tuple-element.4) | data formatting | bytes 4194304
  92.5 0.8 copy.6
Async XLA Ops:
  0.6 1.2 %copy-start = (bf16[512,1024]{1,0:T(8,128)(2,1)S(1)}, bf16[512,1024]{1,0:T(8,128)(2,1)}, u32[]{:S(2)}) copy-start(bf16[512,1024]{1,0:T(8,128)(2,1)} %x_hbm.1) | copy-start | bytes 3145732

commit v4 on v3

--- a/solution.py
+++ b/solution.py
@@ -15,8 +15,10 @@
 LATE = PARTS // 2
 PASS = 2
 USE = 4
-HEAD_START = 6000
-LAST = 2
+HEAD_START = 5000
+TILE = 64
+CLOSE = 4
+END = 3
 MESH = pl.DeviceIdType.MESH
 
 
@@ -79,8 +81,8 @@
     return out
 
 
-def kernel(sizes, x_hbm, win_out, band_out, k_buf, j_buf, b_buf, k_stat, j_stat, b_stat,
-           local_sem, k_recv, up_send, down_send, x_send, j_recv, j_send, b_recv, b_send, w_send, *band_wide):
+def kernel(sizes, x_hbm, win_sum, band_sum, k_stat, j_stat, b_stat, k_buf, j_buf, b_buf,
+           local_sem, k_recv, up_send, down_send, x_send, j_recv, j_send, b_recv, b_send, w_send):
     shard_count, windows, blocks, rows, width, jw, band, bw = sizes
     line = shard_count // COLS
     part_rows = rows // PARTS
@@ -135,7 +137,6 @@
             device_id=to, device_id_type=MESH)
 
     order = plan(line)
-    band_sum = band_wide[0] if band_wide else band_out
     low = z < line // 2
     near_z = jnp.where(low, z, line - 1 - z)
 
@@ -189,7 +190,7 @@
     k_stat[...] = jnp.zeros_like(k_stat)
     j_stat[...] = jnp.zeros_like(j_stat)
     b_stat[...] = jnp.zeros_like(b_stat)
-    win_out[...] = jnp.zeros_like(win_out)
+    win_sum[...] = jnp.zeros_like(win_sum)
     band_sum[...] = jnp.zeros_like(band_sum)
 
     def take(side, zz, c, q):
@@ -278,24 +279,6 @@
                 def _():
                     slice_copy(b_buf.at[q], b_buf, q, b_send.at[b], b_recv, flip(b)).start()
 
-    def ready(q):
-        @pl.when(j_rel[0] != 0)
-        def _():
-            j_arrive(q)
-
-        @pl.when(j_mine)
-        def _():
-            j_buf[q] = k_buf[q, :, pl.ds(j_off, jw)]
-
-        @pl.when(b_rel[0] != 0)
-        def _():
-            b_arrive(q)
-
-        if windows == 1:
-            @pl.when(b_mine)
-            def _():
-                b_buf[q] = k_buf[q, :, pl.ds(b_off, bw)]
-
     def add_stats(stat, block):
         wide = block.astype(jnp.float32).reshape(part_rows // 8, 8, block.shape[-1])
         stat[0] += jnp.sum(wide, axis=0)
@@ -305,23 +288,43 @@
         return lax.dot_general(a, b, (((0,), (0,)), ((), ())), preferred_element_type=jnp.float32)
 
     def compute(q):
-        ready(q)
+        @pl.when(j_rel[0] != 0)
+        def _():
+            j_arrive(q)
+
+        @pl.when(j_mine)
+        def _():
+            j_buf[q] = k_buf[q, :, pl.ds(j_off, jw)]
+
+        @pl.when(b_rel[0] != 0)
+        def _():
+            b_arrive(q)
+
+        if windows == 1:
+            @pl.when(b_mine)
+            def _():
+                b_buf[q] = k_buf[q, :, pl.ds(b_off, bw)]
+
         whole = k_buf[q]
         j_cols = j_buf[q]
         b_cols = b_buf[q]
         add_stats(k_stat, whole)
         add_stats(j_stat, j_cols)
         add_stats(b_stat, b_cols)
-
-        win_out[0] += pair(j_cols, whole)
+        win_sum[0] += pair(j_cols, whole)
         band_sum[0] += pair(b_cols, whole)
 
     def place(o):
         return item(o)[3]
 
+    def each(first, last, what):
+        def one(i, _):
+            what(place(i))
+
+        lax.fori_loop(first, last, one, None)
+
     def summed(o):
-        closing = jnp.maximum(0, o - (chunks - 1 - 2 * (USE - LAST))) // 2
-        return jnp.maximum(0, o + 1 - jnp.maximum(LAST, USE - closing))
+        return jnp.maximum(0, o + 1 - USE)
 
     def step(o, held):
         side, zz, c, q = item(o)
@@ -331,37 +334,29 @@
         def _():
             forward(held[PASS - 1])
 
-        lax.fori_loop(summed(o - 1), summed(o), lambda i, _: compute(place(i)), None)
+        each(summed(o - 1), summed(o), compute)
         return (q, *held[:-1])
 
-    held = lax.fori_loop(0, chunks, step, (jnp.int32(0),) * PASS)
-    for k in reversed(range(PASS)):
-        forward(held[k])
-
-    def rest(i, _):
-        compute(place(i))
-
-    lax.fori_loop(chunks - LAST, chunks, rest, None)
-
-    count = jnp.float32(rows * shard_count)
-
-    def moments(total, square):
-        mean = total / count
-        return mean, 1.0 / jnp.maximum(square / count - mean * mean, VAR_FLOOR)
-
-    row_mean, row_inv = moments(jnp.sum(k_stat[0], axis=0, keepdims=True), jnp.sum(k_stat[1], axis=0, keepdims=True))
-
-    def finish(out, stat, height):
-        mean, inv = moments(jnp.sum(stat[0].T, axis=1, keepdims=True), jnp.sum(stat[1].T, axis=1, keepdims=True))
-        for a in range(0, height, 64):
-            e = min(a + 64, height)
-            covar = out[0, a:e] / count - mean[a:e] * row_mean
-            out[0, a:e] = covar * covar * (inv[a:e] * row_inv)
-
-    finish(win_out, j_stat, jw)
-    finish(band_sum, b_stat, bw)
-    if band_wide:
-        band_out[0] = band_sum[0, pl.ds(pl.multiple_of((s * band) % bw, band), band)]
+    at_end = (z == 0) | (z == line - 1)
+    eager = at_end & (j_home == b_home)
+    closing = chunks - CLOSE
+    lax.fori_loop(0, closing, step, (jnp.int32(0),) * PASS)
+
+    def passed(o):
+        return jnp.where(o < closing, closing - PASS, jnp.where(eager, o, o - 1))
+
+    def summed_in(o):
+        lag = jnp.where(eager, 0, jnp.where(at_end, END, USE))
+        return jnp.where(o < closing, closing - USE, o - lag)
+
+    def close(o, _):
+        each(passed(o - 1), passed(o), forward)
+        each(summed_in(o - 1), summed_in(o), compute)
+        take(*item(o))
+
+    lax.fori_loop(closing, chunks, close, None)
+    each(passed(chunks - 1), chunks, forward)
+    each(summed_in(chunks - 1), chunks, compute)
 
     def sent(buf, number, sem):
         part = buf.at[pl.ds(0, number)]
@@ -392,6 +387,39 @@
         @pl.when(b_mine)
         def _():
             sent(b_buf, chunks, w_send)
+
+
+def finish(sizes, win_sum, band_sum, k_stat, j_stat, b_stat, win_out, band_out, win_buf, band_buf, sems):
+    shard_count, windows, blocks, rows, width, jw, band, bw = sizes
+    count = jnp.float32(rows * shard_count)
+    off = (lax.axis_index("samp") * band) % bw
+
+    def moments(total, square):
+        mean = total / count
+        return mean, 1.0 / jnp.maximum(square / count - mean * mean, VAR_FLOOR)
+
+    row_mean, row_inv = moments(jnp.sum(k_stat[0], axis=0, keepdims=True), jnp.sum(k_stat[1], axis=0, keepdims=True))
+
+    def squares(total, stat, buf, height, copy):
+        mean, inv = moments(jnp.sum(stat[0].T, axis=1, keepdims=True), jnp.sum(stat[1].T, axis=1, keepdims=True))
+        for a in range(0, height, TILE):
+            e = a + TILE
+            covar = total[0, a:e] / count - mean[a:e] * row_mean
+            buf[a:e] = covar * covar * (inv[a:e] * row_inv)
+            copy(a // TILE)
+
+    def win_copy(t):
+        return pltpu.make_async_copy(
+            win_buf.at[pl.ds(t * TILE, TILE)], win_out.at[0, pl.ds(t * TILE, TILE)], sems.at[t])
+
+    band_copy = pltpu.make_async_copy(
+        band_buf.at[pl.ds(pl.multiple_of(off, 8), band)], band_out.at[0], sems.at[jw // TILE])
+    squares(win_sum, j_stat, win_buf, jw, lambda t: win_copy(t).start())
+    squares(band_sum, b_stat, band_buf, bw, lambda t: None)
+    band_copy.start()
+    for t in range(jw // TILE):
+        win_copy(t).wait()
+    band_copy.wait()
 
 
 def shards(dosages):
@@ -407,30 +435,47 @@
     part_rows = rows // PARTS
     sizes = (shard_count, windows, blocks, rows, width, jw, band, bw)
     dma = pltpu.SemaphoreType.DMA
-    return pl.pallas_call(
+    f32 = jnp.float32
+    sums = (
+        jax.ShapeDtypeStruct((1, jw, width), f32),
+        jax.ShapeDtypeStruct((1, bw, width), f32),
+        jax.ShapeDtypeStruct((2, 8, width), f32),
+        jax.ShapeDtypeStruct((2, 8, jw), f32),
+        jax.ShapeDtypeStruct((2, 8, bw), f32),
+    )
+    parts = pl.pallas_call(
         functools.partial(kernel, sizes),
-        out_shape=(
-            jax.ShapeDtypeStruct((1, jw, width), jnp.float32),
-            jax.ShapeDtypeStruct((1, band, width), jnp.float32),
-        ),
+        out_shape=sums,
         in_specs=[pl.BlockSpec(memory_space=pl.ANY)],
-        out_specs=[pl.BlockSpec(memory_space=pltpu.VMEM)] * 2,
+        out_specs=[pl.BlockSpec(memory_space=pltpu.VMEM)] * len(sums),
         scratch_shapes=[
             pltpu.VMEM((chunks, part_rows, width), jnp.bfloat16),
             pltpu.VMEM((chunks, part_rows, jw), jnp.bfloat16),
             pltpu.VMEM((chunks, part_rows, bw), jnp.bfloat16),
-            pltpu.VMEM((2, 8, width), jnp.float32),
-            pltpu.VMEM((2, 8, jw), jnp.float32),
-            pltpu.VMEM((2, 8, bw), jnp.float32),
             dma((PARTS,)),
             dma((chunks,)), dma, dma, dma,
             dma((chunks,)), dma((bits,)),
             dma((chunks,)), dma((bits,)), dma,
-        ] + ([pltpu.VMEM((1, bw, width), jnp.float32)] if bw != band else []),
+        ],
         compiler_params=pltpu.CompilerParams(
             collective_id=0, has_side_effects=True, vmem_limit_bytes=24 * 2**20
         ),
     )(dosages)
+    return pl.pallas_call(
+        functools.partial(finish, sizes),
+        out_shape=(
+            jax.ShapeDtypeStruct((1, jw, width), f32),
+            jax.ShapeDtypeStruct((1, band, width), f32),
+        ),
+        in_specs=[pl.BlockSpec(memory_space=pltpu.VMEM)] * len(sums),
+        out_specs=[pl.BlockSpec(memory_space=pl.ANY)] * 2,
+        scratch_shapes=[
+            pltpu.VMEM((jw, width), f32),
+            pltpu.VMEM((bw, width), f32),
+            dma((jw // TILE + 1,)),
+        ],
+        compiler_params=pltpu.CompilerParams(vmem_limit_bytes=24 * 2**20),
+    )(*parts)
 
 
 def solution(mesh):

time: 94 us -> 93.4 us (level)
  local copies, waits for them, and re-layouts: 3.33 us -> 1.22 us
  Pallas kernels: 89.4 us -> 90.6 us
    unnamed x4 -> x2, local copies, waits for them, and re-layouts: 3.33 us -> 1.22 us
    pallas_call x1 -> x2, Pallas kernels: 89.4 us -> 90.6 us  [the longest x1 88.3 us: shards(): pl.pallas_call(functools.partial(kernel, sizes), out_shape=sums, in_specs...]
where the time goes in v4:
time: 93.4 us; the launch traced here: 92.4 us
  Pallas kernels  90.6 us (97%)
  local copies, waits for them, and re-layouts  1.22 us (1%)
    pallas_call x1, Pallas kernels, shards(): pl.pallas_call(functools.partial(kernel, sizes), out_shape=sums, in_specs...  88.3 us
    pallas_call x1, Pallas kernels, shards(): pl.pallas_call(functools.partial(finish, sizes), out_shape=(jax.ShapeDtyp...  2.27 us

profile of v4, /device:TPU:5, one launch (start us, length us, event | category | flops | bytes accessed | tf_op | source)
XLA Modules:
  0.0 92.4 jit_solution(9326381628208854517)
XLA Ops:
  0.6 0.0 copy-start
  0.6 1.2 %copy-done = bf16[512,1024]{1,0:T(8,128)(2,1)S(1)} copy-done((bf16[512,1024]{1,0:T(8,128)(2,1)S(1)}, bf16[512,1024]{1,0:T(8,128)(2,1)}, u32[]{:S(2)}) %copy-start) | copy-done | bytes 1048600
  1.9 88.3 %shard_map.30 = (f32[1,512,1024]{2,1,0:T(8,128)S(1)}, f32[1,128,1024]{2,1,0:T(8,128)S(1)}, f32[2,8,1024]{2,1,0:T(8,128)S(1)}, f32[2,8,512]{2,1,0:T(8,128)S(1)}, f32[2,8,128]{2,1,0:T(8,128)S(1)}) custom-call(bf16[512,1024]{1,0:T(8,128)(2,1)S(1)} %copy-done), custom_call_target="tpu_custom_call" | custom-call | tf_op jit(solution)/shard_map/pallas_call | solution.py:446
  90.1 2.3 %shard_map.31 = (f32[1,512,1024]{2,1,0:T(8,128)}, f32[1,128,1024]{2,1,0:T(8,128)}) custom-call(f32[1,512,1024]{2,1,0:T(8,128)S(1)} %get-tuple-element.7.win_sum, f32[1,128,1024]{2,1,0:T(8,128)S(1)} %get-tuple-element.8.band_sum, f32[2,8,1024]{2,1,0:T(8,128)S(1)} %get-tuple-element.9.k_stat, f32[2,8,512]{2,1,0:T(8,128)S(1)} %get-tuple-element.10.j_stat, ...), custom_call_target="tpu_custom_call" | custom-call | tf_op jit(solution)/shard_map/pallas_call | solution.py:464
Async XLA Ops:
  0.6 1.2 %copy-start = (bf16[512,1024]{1,0:T(8,128)(2,1)S(1)}, bf16[512,1024]{1,0:T(8,128)(2,1)}, u32[]{:S(2)}) copy-start(bf16[512,1024]{1,0:T(8,128)(2,1)} %x_hbm.1) | copy-start | bytes 3145732

commit v5 on v4

--- a/solution.py
+++ b/solution.py
@@ -15,7 +15,7 @@
 LATE = PARTS // 2
 PASS = 2
 USE = 4
-HEAD_START = 5000
+HEAD_START = 6000
 TILE = 64
 CLOSE = 4
 END = 3
@@ -104,12 +104,18 @@
     def flip(b):
         return {"snp": n + (1 << b) * (1 - 2 * bit(n, b))}
 
+    def beside(delta):
+        to = n
+        for b in range(bits):
+            if delta >> b & 1:
+                to = to + (1 << b) * (1 - 2 * bit(n, b))
+        return {"snp": to}
+
     j_home = (s * jw) // width
     j_off = pl.multiple_of((s * jw) % width, jw)
     b_home = (s * band) // width
     b_off = pl.multiple_of(((s * band) % width) // bw * bw, bw)
     j_rel = [(bit(n, b) + bit(j_home, b)) % 2 for b in range(bits)]
-    b_rel = [(bit(n, b) + bit(b_home, b)) % 2 for b in range(bits)]
 
     def sends_on(rel, b):
         low = jnp.int32(0)
@@ -124,7 +130,7 @@
         return total == 0
 
     j_mine = is_home(j_rel)
-    b_mine = is_home(b_rel)
+    b_mine = n == b_home
 
     def k_copy(q, sem, to):
         return pltpu.make_async_remote_copy(
@@ -173,9 +179,9 @@
     pl.when(has_up)(lambda: greet(up))
     pl.when(has_down)(lambda: greet(down))
     greet(across)
-    for b in range(bits):
-        greet(flip(b))
-    expected = 1 + bits
+    for delta in range(1, blocks):
+        greet(beside(delta))
+    expected = blocks
     if windows > 1:
         w = lax.axis_index("win")
         before = {"win": (w + windows - 1) % windows}
@@ -244,10 +250,12 @@
             def _():
                 slice_copy(k_buf.at[q, :, pl.ds(j_off, jw)], j_buf, q, j_send.at[b], j_recv, flip(b)).start()
 
-            if windows == 1:
-                @pl.when(b_mine)
-                def _():
-                    slice_copy(k_buf.at[q, :, pl.ds(b_off, bw)], b_buf, q, b_send.at[b], b_recv, flip(b)).start()
+        if windows == 1:
+            @pl.when(b_mine)
+            def _():
+                for delta in reversed(range(1, blocks)):
+                    slice_copy(k_buf.at[q, :, pl.ds(b_off, bw)], b_buf, q, b_send.at[delta - 1], b_recv,
+                               beside(delta)).start()
         if windows > 1:
             @pl.when(b_mine)
             def _():
@@ -260,7 +268,6 @@
         slice_copy(k_buf.at[q, :, pl.ds(b_off, bw)], b_buf, q, b_send.at[0], b_recv, flip(0)).wait_recv()
 
     j_passes = (j_rel[0] == 0) & jnp.logical_not(j_mine)
-    b_passes = b_rel[0] == 0 if windows > 1 else (b_rel[0] == 0) & jnp.logical_not(b_mine)
 
     def forward(q):
         @pl.when(j_passes)
@@ -271,13 +278,12 @@
                 def _():
                     slice_copy(j_buf.at[q], j_buf, q, j_send.at[b], j_recv, flip(b)).start()
 
-        @pl.when(b_passes)
-        def _():
-            b_arrive(q)
-            for b in reversed(range(bits)):
-                @pl.when(sends_on(b_rel, b))
-                def _():
-                    slice_copy(b_buf.at[q], b_buf, q, b_send.at[b], b_recv, flip(b)).start()
+        if windows > 1:
+            @pl.when(b_mine)
+            def _():
+                b_arrive(q)
+                for delta in reversed(range(1, blocks)):
+                    slice_copy(b_buf.at[q], b_buf, q, b_send.at[delta - 1], b_recv, beside(delta)).start()
 
     def add_stats(stat, block):
         wide = block.astype(jnp.float32).reshape(part_rows // 8, 8, block.shape[-1])
@@ -296,7 +302,7 @@
         def _():
             j_buf[q] = k_buf[q, :, pl.ds(j_off, jw)]
 
-        @pl.when(b_rel[0] != 0)
+        @pl.when(jnp.logical_not(b_mine))
         def _():
             b_arrive(q)
 
@@ -355,8 +361,11 @@
         take(*item(o))
 
     lax.fori_loop(closing, chunks, close, None)
-    each(passed(chunks - 1), chunks, forward)
-    each(summed_in(chunks - 1), chunks, compute)
+    begun = summed_in(chunks - 1)
+    each(passed(chunks - 1), chunks - 1, forward)
+    each(begun, chunks - 1, compute)
+    each(chunks - 1, chunks, forward)
+    each(chunks - 1, chunks, compute)
 
     def sent(buf, number, sem):
         part = buf.at[pl.ds(0, number)]
@@ -380,12 +389,11 @@
         def _():
             sent(j_buf, chunks, j_send.at[b])
 
-        @pl.when(sends_on(b_rel, b))
-        def _():
-            sent(b_buf, chunks, b_send.at[b])
-    if windows > 1:
-        @pl.when(b_mine)
-        def _():
+    @pl.when(b_mine)
+    def _():
+        for delta in range(1, blocks):
+            sent(b_buf, chunks, b_send.at[delta - 1])
+        if windows > 1:
             sent(b_buf, chunks, w_send)
 
 
@@ -401,7 +409,9 @@
     row_mean, row_inv = moments(jnp.sum(k_stat[0], axis=0, keepdims=True), jnp.sum(k_stat[1], axis=0, keepdims=True))
 
     def squares(total, stat, buf, height, copy):
-        mean, inv = moments(jnp.sum(stat[0].T, axis=1, keepdims=True), jnp.sum(stat[1].T, axis=1, keepdims=True))
+        both = moments(jnp.sum(stat[0], axis=0, keepdims=True), jnp.sum(stat[1], axis=0, keepdims=True))
+        both = jnp.concatenate([both[0]] * 4 + [both[1]] * 4, axis=0).T
+        mean, inv = both[:, 0:1], both[:, 4:5]
         for a in range(0, height, TILE):
             e = a + TILE
             covar = total[0, a:e] / count - mean[a:e] * row_mean
@@ -455,7 +465,7 @@
             dma((PARTS,)),
             dma((chunks,)), dma, dma, dma,
             dma((chunks,)), dma((bits,)),
-            dma((chunks,)), dma((bits,)), dma,
+            dma((chunks,)), dma((blocks - 1,)), dma,
         ],
         compiler_params=pltpu.CompilerParams(
             collective_id=0, has_side_effects=True, vmem_limit_bytes=24 * 2**20

time: 93.4 us -> 91.8 us (0.983)
  Pallas kernels: 90.6 us -> 89 us
    pallas_call x1, Pallas kernels: 88.3 us -> 86.9 us  [shards(): pl.pallas_call(functools.partial(kernel, sizes), out_shape=sums, in_specs...]
where the time goes in v5:
time: 91.8 us; the launch traced here: 90.9 us
  Pallas kernels  89 us (97%)
  local copies, waits for them, and re-layouts  1.22 us (1%)
    pallas_call x1, Pallas kernels, shards(): pl.pallas_call(functools.partial(kernel, sizes), out_shape=sums, in_specs...  86.9 us
    pallas_call x1, Pallas kernels, shards(): pl.pallas_call(functools.partial(finish, sizes), out_shape=(jax.ShapeDtyp...  2.11 us

profile of v5, /device:TPU:5, one launch (start us, length us, event | category | flops | bytes accessed | tf_op | source)
XLA Modules:
  0.0 90.9 jit_solution(3811199717630014081)
XLA Ops:
  0.6 0.0 copy-start
  0.6 1.2 %copy-done = bf16[512,1024]{1,0:T(8,128)(2,1)S(1)} copy-done((bf16[512,1024]{1,0:T(8,128)(2,1)S(1)}, bf16[512,1024]{1,0:T(8,128)(2,1)}, u32[]{:S(2)}) %copy-start) | copy-done | bytes 1048600
  1.9 86.9 %shard_map.30 = (f32[1,512,1024]{2,1,0:T(8,128)S(1)}, f32[1,128,1024]{2,1,0:T(8,128)S(1)}, f32[2,8,1024]{2,1,0:T(8,128)S(1)}, f32[2,8,512]{2,1,0:T(8,128)S(1)}, f32[2,8,128]{2,1,0:T(8,128)S(1)}) custom-call(bf16[512,1024]{1,0:T(8,128)(2,1)S(1)} %copy-done), custom_call_target="tpu_custom_call" | custom-call | tf_op jit(solution)/shard_map/pallas_call | solution.py:456
  88.8 2.1 %shard_map.31 = (f32[1,512,1024]{2,1,0:T(8,128)}, f32[1,128,1024]{2,1,0:T(8,128)}) custom-call(f32[1,512,1024]{2,1,0:T(8,128)S(1)} %get-tuple-element.7.win_sum, f32[1,128,1024]{2,1,0:T(8,128)S(1)} %get-tuple-element.8.band_sum, f32[2,8,1024]{2,1,0:T(8,128)S(1)} %get-tuple-element.9.k_stat, f32[2,8,512]{2,1,0:T(8,128)S(1)} %get-tuple-element.10.j_stat, ...), custom_call_target="tpu_custom_call" | custom-call | tf_op jit(solution)/shard_map/pallas_call | solution.py:474
Async XLA Ops:
  0.6 1.2 %copy-start = (bf16[512,1024]{1,0:T(8,128)(2,1)S(1)}, bf16[512,1024]{1,0:T(8,128)(2,1)}, u32[]{:S(2)}) copy-start(bf16[512,1024]{1,0:T(8,128)(2,1)} %x_hbm.1) | copy-start | bytes 3145732

commit v6 on v5

--- a/solution.py
+++ b/solution.py
@@ -132,9 +132,9 @@
     j_mine = is_home(j_rel)
     b_mine = n == b_home
 
-    def k_copy(q, sem, to):
+    def k_copy(q, sem, to, src=None):
         return pltpu.make_async_remote_copy(
-            src_ref=k_buf.at[q], dst_ref=k_buf.at[q], send_sem=sem, recv_sem=k_recv.at[q],
+            src_ref=k_buf.at[q] if src is None else src, dst_ref=k_buf.at[q], send_sem=sem, recv_sem=k_recv.at[q],
             device_id=to, device_id_type=MESH)
 
     def slice_copy(src, buf, q, send, recv, to):
@@ -204,22 +204,25 @@
 
         @pl.when(mine)
         def _():
-            pltpu.make_async_copy(x_hbm.at[pl.ds(c * part_rows, part_rows)],
-                                  k_buf.at[s * PARTS + c], local_sem.at[c]).wait()
+            own = x_hbm.at[pl.ds(c * part_rows, part_rows)]
+            pl.when(has_up)(lambda: k_copy(q, up_send, up, own).start())
+            pl.when(has_down)(lambda: k_copy(q, down_send, down, own).start())
+            k_copy(q, x_send, across, own).start()
+            pltpu.make_async_copy(own, k_buf.at[q], local_sem.at[c]).wait()
 
         @pl.when(jnp.logical_not(mine))
         def _():
             k_copy(q, x_send, across).wait_recv()
 
-        @pl.when((side == 0) & (zz <= z) & has_up)
+        @pl.when((side == 0) & (zz < z) & has_up)
         def _():
             k_copy(q, up_send, up).start()
 
-        @pl.when((side == 0) & (zz >= z) & has_down)
+        @pl.when((side == 0) & (zz > z) & has_down)
         def _():
             k_copy(q, down_send, down).start()
 
-        @pl.when((side == 0) & jnp.logical_not(skips_x(zz, c)))
+        @pl.when((side == 0) & (zz != z) & jnp.logical_not(skips_x(zz, c)))
         def _():
             k_copy(q, x_send, across).start()
 
@@ -286,14 +289,14 @@
                     slice_copy(b_buf.at[q], b_buf, q, b_send.at[delta - 1], b_recv, beside(delta)).start()
 
     def add_stats(stat, block):
-        wide = block.astype(jnp.float32).reshape(part_rows // 8, 8, block.shape[-1])
+        wide = block.astype(jnp.float32).reshape(block.shape[0] // 8, 8, block.shape[-1])
         stat[0] += jnp.sum(wide, axis=0)
         stat[1] += jnp.sum(wide * wide, axis=0)
 
     def pair(a, b):
         return lax.dot_general(a, b, (((0,), (0,)), ((), ())), preferred_element_type=jnp.float32)
 
-    def compute(q):
+    def arrive(q):
         @pl.when(j_rel[0] != 0)
         def _():
             j_arrive(q)
@@ -311,9 +314,11 @@
             def _():
                 b_buf[q] = k_buf[q, :, pl.ds(b_off, bw)]
 
-        whole = k_buf[q]
-        j_cols = j_buf[q]
-        b_cols = b_buf[q]
+    def compute(*places):
+        for q in places:
+            arrive(q)
+        whole, j_cols, b_cols = (
+            jnp.concatenate([buf[q] for q in places], axis=0) for buf in (k_buf, j_buf, b_buf))
         add_stats(k_stat, whole)
         add_stats(j_stat, j_cols)
         add_stats(b_stat, b_cols)
@@ -353,7 +358,8 @@
 
     def summed_in(o):
         lag = jnp.where(eager, 0, jnp.where(at_end, END, USE))
-        return jnp.where(o < closing, closing - USE, o - lag)
+        last = jnp.where(eager, chunks - 2, chunks - 4)
+        return jnp.where(o < closing, closing - USE, jnp.where(o == chunks - 1, last, o - lag))
 
     def close(o, _):
         each(passed(o - 1), passed(o), forward)
@@ -361,11 +367,13 @@
         take(*item(o))
 
     lax.fori_loop(closing, chunks, close, None)
-    begun = summed_in(chunks - 1)
+    def two(i, _):
+        compute(place(2 * i), place(2 * i + 1))
+
     each(passed(chunks - 1), chunks - 1, forward)
-    each(begun, chunks - 1, compute)
+    lax.fori_loop(summed_in(chunks - 1) // 2, chunks // 2 - 1, two, None)
     each(chunks - 1, chunks, forward)
-    each(chunks - 1, chunks, compute)
+    lax.fori_loop(chunks // 2 - 1, chunks // 2, two, None)
 
     def sent(buf, number, sem):
         part = buf.at[pl.ds(0, number)]

time: 91.8 us -> 91.5 us (level)
  no operation moved by 1% of the time
where the time goes in v6:
time: 91.5 us; the launch traced here: 90.9 us
  Pallas kernels  89.1 us (97%)
  local copies, waits for them, and re-layouts  1.22 us (1%)
    pallas_call x1, Pallas kernels, shards(): pl.pallas_call(functools.partial(kernel, sizes), out_shape=sums, in_specs...  87 us
    pallas_call x1, Pallas kernels, shards(): pl.pallas_call(functools.partial(finish, sizes), out_shape=(jax.ShapeDtyp...  2.11 us

profile of v6, /device:TPU:5, one launch (start us, length us, event | category | flops | bytes accessed | tf_op | source)
XLA Modules:
  0.0 90.9 jit_solution(15967608219756486704)
XLA Ops:
  0.6 0.0 copy-start
  0.6 1.2 %copy-done = bf16[512,1024]{1,0:T(8,128)(2,1)S(1)} copy-done((bf16[512,1024]{1,0:T(8,128)(2,1)S(1)}, bf16[512,1024]{1,0:T(8,128)(2,1)}, u32[]{:S(2)}) %copy-start) | copy-done | bytes 1048600
  1.9 87.0 %shard_map.30 = (f32[1,512,1024]{2,1,0:T(8,128)S(1)}, f32[1,128,1024]{2,1,0:T(8,128)S(1)}, f32[2,8,1024]{2,1,0:T(8,128)S(1)}, f32[2,8,512]{2,1,0:T(8,128)S(1)}, f32[2,8,128]{2,1,0:T(8,128)S(1)}) custom-call(bf16[512,1024]{1,0:T(8,128)(2,1)S(1)} %copy-done), custom_call_target="tpu_custom_call" | custom-call | tf_op jit(solution)/shard_map/pallas_call | solution.py:464
  88.8 2.1 %shard_map.31 = (f32[1,512,1024]{2,1,0:T(8,128)}, f32[1,128,1024]{2,1,0:T(8,128)}) custom-call(f32[1,512,1024]{2,1,0:T(8,128)S(1)} %get-tuple-element.7.win_sum, f32[1,128,1024]{2,1,0:T(8,128)S(1)} %get-tuple-element.8.band_sum, f32[2,8,1024]{2,1,0:T(8,128)S(1)} %get-tuple-element.9.k_stat, f32[2,8,512]{2,1,0:T(8,128)S(1)} %get-tuple-element.10.j_stat, ...), custom_call_target="tpu_custom_call" | custom-call | tf_op jit(solution)/shard_map/pallas_call | solution.py:482
Async XLA Ops:
  0.6 1.2 %copy-start = (bf16[512,1024]{1,0:T(8,128)(2,1)S(1)}, bf16[512,1024]{1,0:T(8,128)(2,1)}, u32[]{:S(2)}) copy-start(bf16[512,1024]{1,0:T(8,128)(2,1)} %x_hbm.1) | copy-start | bytes 3145732

commit v7 on v6

--- a/solution.py
+++ b/solution.py
@@ -18,7 +18,7 @@
 HEAD_START = 6000
 TILE = 64
 CLOSE = 4
-END = 3
+END = 2
 MESH = pl.DeviceIdType.MESH
 
 
@@ -334,6 +334,12 @@
 
         lax.fori_loop(first, last, one, None)
 
+    def two(i, _):
+        compute(place(2 * i), place(2 * i + 1))
+
+    def add_up(first, last):
+        lax.fori_loop(first // 2, last // 2, two, None)
+
     def summed(o):
         return jnp.maximum(0, o + 1 - USE)
 
@@ -345,7 +351,7 @@
         def _():
             forward(held[PASS - 1])
 
-        each(summed(o - 1), summed(o), compute)
+        add_up(summed(o - 1), summed(o))
         return (q, *held[:-1])
 
     at_end = (z == 0) | (z == line - 1)
@@ -363,17 +369,14 @@
 
     def close(o, _):
         each(passed(o - 1), passed(o), forward)
-        each(summed_in(o - 1), summed_in(o), compute)
+        add_up(summed_in(o - 1), summed_in(o))
         take(*item(o))
 
     lax.fori_loop(closing, chunks, close, None)
-    def two(i, _):
-        compute(place(2 * i), place(2 * i + 1))
-
     each(passed(chunks - 1), chunks - 1, forward)
-    lax.fori_loop(summed_in(chunks - 1) // 2, chunks // 2 - 1, two, None)
+    add_up(summed_in(chunks - 1), chunks - 2)
     each(chunks - 1, chunks, forward)
-    lax.fori_loop(chunks // 2 - 1, chunks // 2, two, None)
+    add_up(chunks - 2, chunks)
 
     def sent(buf, number, sem):
         part = buf.at[pl.ds(0, number)]

time: 91.5 us -> 91.4 us (level)
  no operation moved by 1% of the time
where the time goes in v7:
time: 91.4 us; the launch traced here: 90.9 us
  Pallas kernels  89.1 us (97%)
  local copies, waits for them, and re-layouts  1.22 us (1%)
    pallas_call x1, Pallas kernels, shards(): pl.pallas_call(functools.partial(kernel, sizes), out_shape=sums, in_specs...  87 us
    pallas_call x1, Pallas kernels, shards(): pl.pallas_call(functools.partial(finish, sizes), out_shape=(jax.ShapeDtyp...  2.11 us

profile of v7, /device:TPU:5, one launch (start us, length us, event | category | flops | bytes accessed | tf_op | source)
XLA Modules:
  0.0 90.9 jit_solution(12486025386503986013)
XLA Ops:
  0.6 0.0 copy-start
  0.6 1.2 %copy-done = bf16[512,1024]{1,0:T(8,128)(2,1)S(1)} copy-done((bf16[512,1024]{1,0:T(8,128)(2,1)S(1)}, bf16[512,1024]{1,0:T(8,128)(2,1)}, u32[]{:S(2)}) %copy-start) | copy-done | bytes 1048600
  1.9 87.0 %shard_map.30 = (f32[1,512,1024]{2,1,0:T(8,128)S(1)}, f32[1,128,1024]{2,1,0:T(8,128)S(1)}, f32[2,8,1024]{2,1,0:T(8,128)S(1)}, f32[2,8,512]{2,1,0:T(8,128)S(1)}, f32[2,8,128]{2,1,0:T(8,128)S(1)}) custom-call(bf16[512,1024]{1,0:T(8,128)(2,1)S(1)} %copy-done), custom_call_target="tpu_custom_call" | custom-call | tf_op jit(solution)/shard_map/pallas_call | solution.py:467
  88.8 2.1 %shard_map.31 = (f32[1,512,1024]{2,1,0:T(8,128)}, f32[1,128,1024]{2,1,0:T(8,128)}) custom-call(f32[1,512,1024]{2,1,0:T(8,128)S(1)} %get-tuple-element.7.win_sum, f32[1,128,1024]{2,1,0:T(8,128)S(1)} %get-tuple-element.8.band_sum, f32[2,8,1024]{2,1,0:T(8,128)S(1)} %get-tuple-element.9.k_stat, f32[2,8,512]{2,1,0:T(8,128)S(1)} %get-tuple-element.10.j_stat, ...), custom_call_target="tpu_custom_call" | custom-call | tf_op jit(solution)/shard_map/pallas_call | solution.py:485
Async XLA Ops:
  0.6 1.2 %copy-start = (bf16[512,1024]{1,0:T(8,128)(2,1)S(1)}, bf16[512,1024]{1,0:T(8,128)(2,1)}, u32[]{:S(2)}) copy-start(bf16[512,1024]{1,0:T(8,128)(2,1)} %x_hbm.1) | copy-start | bytes 3145732

commit v8 on v7

--- a/solution.py
+++ b/solution.py
@@ -375,8 +375,6 @@
     lax.fori_loop(closing, chunks, close, None)
     each(passed(chunks - 1), chunks - 1, forward)
     add_up(summed_in(chunks - 1), chunks - 2)
-    each(chunks - 1, chunks, forward)
-    add_up(chunks - 2, chunks)
 
     def sent(buf, number, sem):
         part = buf.at[pl.ds(0, number)]
@@ -394,6 +392,9 @@
             if zz > 0:
                 sent(k_buf, (line - zz) * PARTS + PARTS - LATE, down_send)
             sent(k_buf, over, x_send)
+
+    each(chunks - 1, chunks, forward)
+    add_up(chunks - 2, chunks)
 
     for b in range(bits):
         @pl.when(sends_on(j_rel, b))

time: 91.4 us -> 91.4 us (level)
  no operation moved by 1% of the time
where the time goes in v8:
time: 91.4 us; the launch traced here: 90.9 us
  Pallas kernels  89.1 us (97%)
  local copies, waits for them, and re-layouts  1.22 us (1%)
    pallas_call x1, Pallas kernels, shards(): pl.pallas_call(functools.partial(kernel, sizes), out_shape=sums, in_specs...  87 us
    pallas_call x1, Pallas kernels, shards(): pl.pallas_call(functools.partial(finish, sizes), out_shape=(jax.ShapeDtyp...  2.11 us

profile of v8, /device:TPU:5, one launch (start us, length us, event | category | flops | bytes accessed | tf_op | source)
XLA Modules:
  0.0 90.9 jit_solution(10553341203491099137)
XLA Ops:
  0.6 0.0 copy-start
  0.6 1.2 %copy-done = bf16[512,1024]{1,0:T(8,128)(2,1)S(1)} copy-done((bf16[512,1024]{1,0:T(8,128)(2,1)S(1)}, bf16[512,1024]{1,0:T(8,128)(2,1)}, u32[]{:S(2)}) %copy-start) | copy-done | bytes 1048600
  1.9 87.0 %shard_map.30 = (f32[1,512,1024]{2,1,0:T(8,128)S(1)}, f32[1,128,1024]{2,1,0:T(8,128)S(1)}, f32[2,8,1024]{2,1,0:T(8,128)S(1)}, f32[2,8,512]{2,1,0:T(8,128)S(1)}, f32[2,8,128]{2,1,0:T(8,128)S(1)}) custom-call(bf16[512,1024]{1,0:T(8,128)(2,1)S(1)} %copy-done), custom_call_target="tpu_custom_call" | custom-call | tf_op jit(solution)/shard_map/pallas_call | solution.py:468
  88.8 2.1 %shard_map.31 = (f32[1,512,1024]{2,1,0:T(8,128)}, f32[1,128,1024]{2,1,0:T(8,128)}) custom-call(f32[1,512,1024]{2,1,0:T(8,128)S(1)} %get-tuple-element.7.win_sum, f32[1,128,1024]{2,1,0:T(8,128)S(1)} %get-tuple-element.8.band_sum, f32[2,8,1024]{2,1,0:T(8,128)S(1)} %get-tuple-element.9.k_stat, f32[2,8,512]{2,1,0:T(8,128)S(1)} %get-tuple-element.10.j_stat, ...), custom_call_target="tpu_custom_call" | custom-call | tf_op jit(solution)/shard_map/pallas_call | solution.py:486
Async XLA Ops:
  0.6 1.2 %copy-start = (bf16[512,1024]{1,0:T(8,128)(2,1)S(1)}, bf16[512,1024]{1,0:T(8,128)(2,1)}, u32[]{:S(2)}) copy-start(bf16[512,1024]{1,0:T(8,128)(2,1)} %x_hbm.1) | copy-start | bytes 3145732

commit v9 on v8

--- a/solution.py
+++ b/solution.py
@@ -15,7 +15,7 @@
 LATE = PARTS // 2
 PASS = 2
 USE = 4
-HEAD_START = 6000
+HEAD_START = 5700
 TILE = 64
 CLOSE = 4
 END = 2

time: 91.4 us -> 91.4 us (level)
  no operation moved by 1% of the time
where the time goes in v9:
time: 91.4 us; the launch traced here: 91.2 us
  Pallas kernels  89.4 us (98%)
  local copies, waits for them, and re-layouts  1.22 us (1%)
    pallas_call x1, Pallas kernels, shards(): pl.pallas_call(functools.partial(kernel, sizes), out_shape=sums, in_specs...  87.3 us
    pallas_call x1, Pallas kernels, shards(): pl.pallas_call(functools.partial(finish, sizes), out_shape=(jax.ShapeDtyp...  2.11 us

profile of v9, /device:TPU:5, one launch (start us, length us, event | category | flops | bytes accessed | tf_op | source)
XLA Modules:
  0.0 91.2 jit_solution(16308065045251819979)
XLA Ops:
  0.6 0.0 copy-start
  0.6 1.2 %copy-done = bf16[512,1024]{1,0:T(8,128)(2,1)S(1)} copy-done((bf16[512,1024]{1,0:T(8,128)(2,1)S(1)}, bf16[512,1024]{1,0:T(8,128)(2,1)}, u32[]{:S(2)}) %copy-start) | copy-done | bytes 1048600
  1.9 87.3 %shard_map.30 = (f32[1,512,1024]{2,1,0:T(8,128)S(1)}, f32[1,128,1024]{2,1,0:T(8,128)S(1)}, f32[2,8,1024]{2,1,0:T(8,128)S(1)}, f32[2,8,512]{2,1,0:T(8,128)S(1)}, f32[2,8,128]{2,1,0:T(8,128)S(1)}) custom-call(bf16[512,1024]{1,0:T(8,128)(2,1)S(1)} %copy-done), custom_call_target="tpu_custom_call" | custom-call | tf_op jit(solution)/shard_map/pallas_call | solution.py:468
  89.1 2.1 %shard_map.31 = (f32[1,512,1024]{2,1,0:T(8,128)}, f32[1,128,1024]{2,1,0:T(8,128)}) custom-call(f32[1,512,1024]{2,1,0:T(8,128)S(1)} %get-tuple-element.7.win_sum, f32[1,128,1024]{2,1,0:T(8,128)S(1)} %get-tuple-element.8.band_sum, f32[2,8,1024]{2,1,0:T(8,128)S(1)} %get-tuple-element.9.k_stat, f32[2,8,512]{2,1,0:T(8,128)S(1)} %get-tuple-element.10.j_stat, ...), custom_call_target="tpu_custom_call" | custom-call | tf_op jit(solution)/shard_map/pallas_call | solution.py:486
Async XLA Ops:
  0.6 1.2 %copy-start = (bf16[512,1024]{1,0:T(8,128)(2,1)S(1)}, bf16[512,1024]{1,0:T(8,128)(2,1)}, u32[]{:S(2)}) copy-start(bf16[512,1024]{1,0:T(8,128)(2,1)} %x_hbm.1) | copy-start | bytes 3145732
